TPU v7x, 32 devices: a whole 2x2x4 slice. The times are simulated.
32 devices in a mesh: src: 4 (over y, x), blk: 8 (over z, core).
Axes of the slice: x: 2, y: 2, z: 4, core: 2. Of those that a mesh axis runs over, the one named last changes fastest.
Arguments:
- values: float32 [4, 512, 32, 128], P('src', 'blk'), may hold values from -0.25 to 0.25
- diagonal: float32 [4, 512, 128], P('src', 'blk'), may hold values from 0.55 to 0.95
- rhs_parts: float32 [4, 512, 128], P('src', 'blk'), may hold values from -24 to 24
- owner_map: int32 [512, 128], P('blk'), may hold values from 0 to 3
- columns: int32 [512, 32, 128], P('blk'), may hold values from 0 to 1073741823
- destination: int32 [512, 1], P('blk'), may hold values from 0 to 7; in each aligned block of 64 rows (0 to 63, 64 to 127, ...) at most 16 rows name the same one
- order_keys: int32 [512], P('blk'), may hold values from 0 to 511, each once
Outputs:
- solution: float32 [512, 128], P('blk')
Inputs may be any that keep to these rules, and one draw needn't show every extreme that they name: `destination`: among the row blocks of one index of blk no owner is named more than 16 times, some owner is named exactly 16 times, and every owner is named by some block. `order_keys`: each key appears once.
All inputs are finite; a program needn't handle non-finite values.
Results may differ from a plain program's by a relative error of at most 0.0003.
Values sent between devices are 32-bit elements; how exact they have to be, the bound alone decides.
A program may use at most 64 MiB of HBM per device.

v0:
```python
import jax
import jax.numpy as jnp
from jax import lax
from jax.sharding import PartitionSpec as P

SWEEPS = 3


def tile_matrix(block_vals, block_cols, tile_rows):
    slot_count = block_vals.shape[0]
    stored = block_vals.shape[1]
    groups = 8
    lanes = jnp.remainder(block_cols, 2 * tile_rows)
    targets = jnp.arange(2 * tile_rows, dtype=jnp.int32)
    grouped_vals = block_vals.reshape(groups, slot_count // groups, stored, tile_rows)
    grouped_lanes = lanes.reshape(groups, slot_count // groups, stored, tile_rows)

    def build(pair):
        group_vals, group_lanes = pair
        picked = jnp.where(group_lanes[..., None] == targets, group_vals[..., None], 0.0)
        return jnp.sum(picked, axis=1)

    dense = lax.map(build, (grouped_vals, grouped_lanes))
    return dense.reshape(slot_count, tile_rows, 2 * tile_rows)


def on_device(values, diagonal, rhs_parts, owner_map, columns, destination, order_keys):
    owners = lax.axis_size("blk")
    part_count = lax.axis_size("src")
    tile_count = destination.shape[0]
    stored = values.shape[2]
    tile_rows = values.shape[3]
    per_peer = 2 * tile_count // owners
    slot_count = owners * per_peer
    owner_of = destination[:, 0]
    tile_ids = jnp.arange(tile_count, dtype=jnp.int32)
    slot_ids = jnp.arange(slot_count, dtype=jnp.int32)
    earlier = (owner_of[None, :] == owner_of[:, None]) & (tile_ids[None, :] < tile_ids[:, None])
    position = jnp.sum(earlier, axis=1)
    slot_of = owner_of * per_peer + position
    slot_hits = slot_of[None, :] == slot_ids[:, None]
    filled = jnp.any(slot_hits, axis=1)
    source_tile = jnp.sum(jnp.where(slot_hits, tile_ids[None, :], 0), axis=1)
    is_owned = owner_map == lax.axis_index("src")
    own_rhs = jnp.where(is_owned, rhs_parts[0], 0.0)
    send_vals = jnp.where(filled[:, None, None], values[0][source_tile], 0.0)
    send_diag = jnp.where(filled[:, None], diagonal[0][source_tile], 0.0)
    send_rhs = jnp.where(filled[:, None], own_rhs[source_tile], 0.0)
    send_cols = columns[source_tile]
    send_keys = jnp.where(filled, order_keys[source_tile], -1)
    quarter = stored // part_count
    part_vals = lax.psum_scatter(send_vals, "src", scatter_dimension=1, tiled=True)
    sum_diag, sum_rhs = lax.psum((send_diag, send_rhs), "src")
    part_cols = lax.dynamic_slice_in_dim(send_cols, lax.axis_index("src") * quarter, quarter, 1)
    got_vals, got_diag, got_rhs = (
        lax.all_to_all(part_vals, "blk", split_axis=0, concat_axis=0, tiled=True),
        lax.all_to_all(sum_diag, "blk", split_axis=0, concat_axis=0, tiled=True),
        lax.all_to_all(sum_rhs, "blk", split_axis=0, concat_axis=0, tiled=True),
    )
    got_cols, got_keys = (
        lax.all_to_all(part_cols, "blk", split_axis=0, concat_axis=0, tiled=True),
        lax.all_to_all(send_keys, "blk", split_axis=0, concat_axis=0, tiled=True),
    )
    is_live = got_keys >= 0
    tile_total = jnp.sum(is_live)
    smaller = is_live[None, :] & (got_keys[None, :] < got_keys[:, None])
    tile_rank = jnp.sum(smaller, axis=1)
    rank_hits = is_live[None, :] & (tile_rank[None, :] == slot_ids[:, None])
    holder = jnp.sum(jnp.where(rank_hits, slot_ids[None, :], 0), axis=1)
    occupied = slot_ids < tile_total
    block_vals = jnp.where(occupied[:, None, None], got_vals[holder], 0.0)
    block_cols = got_cols[holder]
    right_side = jnp.where(occupied[:, None], got_rhs[holder], 0.0)
    block_diag = jnp.where(occupied[:, None], got_diag[holder], 1.0)
    dense = tile_matrix(block_vals, block_cols, tile_rows)
    following = jnp.remainder(slot_ids + 1, tile_total)
    iterate = jnp.zeros((slot_count, tile_rows), jnp.float32)
    for sweep_index in range(SWEEPS):
        nearby = jnp.concatenate([iterate, iterate[following]], axis=1)
        partial_sum = jnp.sum(dense * nearby[:, None, :], axis=2)
        summed = lax.psum(partial_sum, "src")
        iterate = jnp.where(occupied[:, None], (right_side - summed) / block_diag, 0.0)
    in_slots = jnp.where(is_live[:, None], iterate[tile_rank], 0.0)
    returned = lax.all_to_all(in_slots, "blk", split_axis=0, concat_axis=0, tiled=True)
    return returned[slot_of]


def solution(mesh):
    placed = (
        P("src", "blk", None, None),
        P("src", "blk", None),
        P("src", "blk", None),
        P("blk", None),
        P("blk", None, None),
        P("blk", None),
        P("blk"),
    )
    return jax.shard_map(
        on_device, mesh=mesh, in_specs=placed, out_specs=P("blk", None), check_vma=False
    )
```

profile of v0, /device:TPU:0, one launch (start us, length us, event | category | flops | bytes accessed | tf_op | source)
XLA Modules:
  0.0 320.4 jit_solution(3956767261336183481)
XLA Ops:
  6.6 0.9 convert_reduce_fusion.1
  7.5 0.7 multiply_add_fusion
  8.4 0.8 gather_fusion.5
  9.2 1.6 broadcast_select_fusion
  10.8 1.6 gather_fusion
  12.4 0.7 select_n.147
  13.1 6.4 %all-to-all-start = ((s32[8,16,1]{1,2,0:T(1,128)}), s32[8,16,1]{1,2,0:T(1,128)S(1)}, u32[]{:S(2)}, u32[]{:S(2)}) async-start(s32[8,16,1]{1,2,0:T(1,128)} %bitcast.3), calls=%async_computation | async-start | bytes 8192 | tf_op jit(solution)/shard_map/all_to_all | solution.py:62
  19.4 2.2 gather_fusion.3
  21.6 0.9 constant_dynamic-slice_fusion
  22.5 2.4 all-to-all-done
  24.9 3.5 %all-to-all-start.2 = ((s32[128,8,128]{2,1,0:T(8,128)}), s32[128,8,128]{2,1,0:T(8,128)S(1)}, u32[]{:S(2)}, u32[]{:S(2)}) async-start(s32[128,8,128]{2,1,0:T(8,128)} %constant_dynamic-slice_fusion), calls=%async_computation.2 | async-start | bytes 1048576 | tf_op jit(solution)/shard_map/all_to_all | solution.py:61
  28.5 0.6 gather_fusion.1
  29.1 0.6 gather_fusion.8
  29.8 0.7 broadcast_select_fusion.4
  30.5 0.5 broadcast.232
  31.0 0.7 reduce.7
  31.8 0.6 convert_reduce_fusion.2
  33.9 0.6 gather_fusion.7
  34.5 9.2 %all-to-all-done.2 = s32[128,8,128]{2,1,0:T(8,128)S(1)} async-done(((s32[128,8,128]{2,1,0:T(8,128)}), s32[128,8,128]{2,1,0:T(8,128)S(1)}, u32[]{:S(2)}, u32[]{:S(2)}) %all-to-all-start.2) | async-done | bytes 524320 | tf_op jit(solution)/shard_map/all_to_all | solution.py:61
  43.7 5.2 %reduce-scatter.2.cloned.1.call-done = f32[128,8,128]{2,1,0:T(8,128)} async-done(((f32[128,32,128]{2,1,0:T(8,128)}), f32[128,8,128]{2,1,0:T(8,128)}) %reduce-scatter.2.cloned.1.call-update) | async-done | bytes 524304 | tf_op jit(solution)/shard_map/reduce_scatter | solution.py:52
  48.9 4.6 %all-to-all-start.3 = ((f32[128,8,128]{2,1,0:T(8,128)}), f32[128,8,128]{2,1,0:T(8,128)S(1)}, u32[]{:S(2)}, u32[]{:S(2)}) async-start(f32[128,8,128]{2,1,0:T(8,128)} %reduce-scatter.2.cloned.1.call-done), calls=%async_computation.4 | async-start | bytes 1048576 | tf_op jit(solution)/shard_map/all_to_all | solution.py:56
  53.5 0.7 add_compare_fusion
  54.5 0.8 gather_fusion.4
  55.5 13.3 %all-to-all-done.3 = f32[128,8,128]{2,1,0:T(8,128)S(1)} async-done(((f32[128,8,128]{2,1,0:T(8,128)}), f32[128,8,128]{2,1,0:T(8,128)S(1)}, u32[]{:S(2)}, u32[]{:S(2)}) %all-to-all-start.3) | async-done | bytes 524320 | tf_op jit(solution)/shard_map/all_to_all | solution.py:56
  68.8 0.8 gather_fusion.6
  69.8 57.8 %while.11 = (s32[]{:T(128)}, f32[8,16,128,256]{3,2,1,0:T(8,128)}, s32[8,16,8,128]{3,2,1,0:T(8,128)S(1)}, f32[8,16,8,128]{3,2,1,0:T(8,128)S(1)}, s32[]{:T(128)}) while((s32[]{:T(128)}, f32[8,16,128,256]{3,2,1,0:T(8,128)}, s32[8,16,8,128]{3,2,1,0:T(8,128)S(1)}, f32[8,16,8,128]{3,2,1,0:T(8,128)S(1)}, s32[]{:T(128)}) %tuple.23), condition=%wide.region_10.11_spmd.clone, body=%wide.region_8.10_spmd.clone.sunk | while | flops 12058626 | bytes 6685253 | solution.py:23
  69.8 5.7 %select_reduce_fusion.4 = f32[16,128,256]{2,1,0:T(8,128)S(1)} fusion(f32[16,8,128]{2,1,0:T(8,128)S(1)} %dynamic-slice_bitcast_fusion.4, s32[16,8,128]{2,1,0:T(8,128)S(1)} %dynamic-slice_bitcast_fusion.5), kind=kLoop, calls=%fused_computation.16.clone.1 | loop fusion | flops 12058624 | bytes 2228224 | tf_op jit(solution)/shard_map/while/body/eval_jaxpr/reduce_sum | solution.py:21
  75.5 1.6 bitcast_dynamic-update-slice_fusion.2
  77.1 5.7 %select_reduce_fusion.4 = f32[16,128,256]{2,1,0:T(8,128)S(1)} fusion(f32[16,8,128]{2,1,0:T(8,128)S(1)} %dynamic-slice_bitcast_fusion.4, s32[16,8,128]{2,1,0:T(8,128)S(1)} %dynamic-slice_bitcast_fusion.5), kind=kLoop, calls=%fused_computation.16.clone.1 | loop fusion | flops 12058624 | bytes 2228224 | tf_op jit(solution)/shard_map/while/body/eval_jaxpr/reduce_sum | solution.py:21
  82.7 1.5 bitcast_dynamic-update-slice_fusion.2
  84.2 5.7 %select_reduce_fusion.4 = f32[16,128,256]{2,1,0:T(8,128)S(1)} fusion(f32[16,8,128]{2,1,0:T(8,128)S(1)} %dynamic-slice_bitcast_fusion.4, s32[16,8,128]{2,1,0:T(8,128)S(1)} %dynamic-slice_bitcast_fusion.5), kind=kLoop, calls=%fused_computation.16.clone.1 | loop fusion | flops 12058624 | bytes 2228224 | tf_op jit(solution)/shard_map/while/body/eval_jaxpr/reduce_sum | solution.py:21
  89.9 1.5 bitcast_dynamic-update-slice_fusion.2
  91.5 5.7 %select_reduce_fusion.4 = f32[16,128,256]{2,1,0:T(8,128)S(1)} fusion(f32[16,8,128]{2,1,0:T(8,128)S(1)} %dynamic-slice_bitcast_fusion.4, s32[16,8,128]{2,1,0:T(8,128)S(1)} %dynamic-slice_bitcast_fusion.5), kind=kLoop, calls=%fused_computation.16.clone.1 | loop fusion | flops 12058624 | bytes 2228224 | tf_op jit(solution)/shard_map/while/body/eval_jaxpr/reduce_sum | solution.py:21
  97.1 1.5 bitcast_dynamic-update-slice_fusion.2
  98.7 5.7 %select_reduce_fusion.4 = f32[16,128,256]{2,1,0:T(8,128)S(1)} fusion(f32[16,8,128]{2,1,0:T(8,128)S(1)} %dynamic-slice_bitcast_fusion.4, s32[16,8,128]{2,1,0:T(8,128)S(1)} %dynamic-slice_bitcast_fusion.5), kind=kLoop, calls=%fused_computation.16.clone.1 | loop fusion | flops 12058624 | bytes 2228224 | tf_op jit(solution)/shard_map/while/body/eval_jaxpr/reduce_sum | solution.py:21
  104.4 1.6 bitcast_dynamic-update-slice_fusion.2
  106.0 5.7 %select_reduce_fusion.4 = f32[16,128,256]{2,1,0:T(8,128)S(1)} fusion(f32[16,8,128]{2,1,0:T(8,128)S(1)} %dynamic-slice_bitcast_fusion.4, s32[16,8,128]{2,1,0:T(8,128)S(1)} %dynamic-slice_bitcast_fusion.5), kind=kLoop, calls=%fused_computation.16.clone.1 | loop fusion | flops 12058624 | bytes 2228224 | tf_op jit(solution)/shard_map/while/body/eval_jaxpr/reduce_sum | solution.py:21
  111.6 1.5 bitcast_dynamic-update-slice_fusion.2
  113.1 5.7 %select_reduce_fusion.4 = f32[16,128,256]{2,1,0:T(8,128)S(1)} fusion(f32[16,8,128]{2,1,0:T(8,128)S(1)} %dynamic-slice_bitcast_fusion.4, s32[16,8,128]{2,1,0:T(8,128)S(1)} %dynamic-slice_bitcast_fusion.5), kind=kLoop, calls=%fused_computation.16.clone.1 | loop fusion | flops 12058624 | bytes 2228224 | tf_op jit(solution)/shard_map/while/body/eval_jaxpr/reduce_sum | solution.py:21
  118.8 1.6 bitcast_dynamic-update-slice_fusion.2
  120.4 5.7 %select_reduce_fusion.4 = f32[16,128,256]{2,1,0:T(8,128)S(1)} fusion(f32[16,8,128]{2,1,0:T(8,128)S(1)} %dynamic-slice_bitcast_fusion.4, s32[16,8,128]{2,1,0:T(8,128)S(1)} %dynamic-slice_bitcast_fusion.5), kind=kLoop, calls=%fused_computation.16.clone.1 | loop fusion | flops 12058624 | bytes 2228224 | tf_op jit(solution)/shard_map/while/body/eval_jaxpr/reduce_sum | solution.py:21
  126.1 1.5 bitcast_dynamic-update-slice_fusion.2
  127.6 8.6 %multiply_reduce_fusion.2 = f32[8,16,128]{2,1,0:T(8,128)} fusion(f32[8,16,128,256]{3,2,1,0:T(8,128)} %get-tuple-element.32, f32[8,16,256]{2,1,0:T(8,128)S(1)} %bitcast.63), kind=kLoop, calls=%fused_computation.22 | loop fusion | flops 8372224 | bytes 16973824 | tf_op jit(solution)/shard_map/reduce_sum | solution.py:80
  136.2 41.3 %all-reduce.10.cloned.1.call-done = (f32[128,128]{1,0:T(8,128)}, f32[8,16,128]{2,1,0:T(8,128)}, f32[8,16,128]{2,1,0:T(8,128)}) async-done(((f32[128,128]{1,0:T(8,128)}, f32[8,16,128]{2,1,0:T(8,128)}, f32[8,16,128]{2,1,0:T(8,128)}), (f32[128,128]{1,0:T(8,128)}, f32[8,16,128]{2,1,0:T(8,128)}, f32[8,16,128]{2,1,0:T(8,128)})) %all-reduce.10.cloned.1.call-update) | async-done | bytes 196624 | tf_op jit(solution)/shard_map/psum | solution.py:81
  177.5 10.5 %all_to_all.52 = f32[8,16,128]{2,1,0:T(8,128)S(1)} all-to-all(f32[8,16,128]{2,1,0:T(8,128)} %get-tuple-element.53), channel_id=1, replica_groups=mesh['src'=4,'blk'=8] {'blk'}, dimensions={0} | all-to-all | bytes 131072 | tf_op jit(solution)/shard_map/all_to_all | solution.py:58
  188.0 3.3 %all-to-all-start.4 = ((f32[8,16,128]{2,1,0:T(8,128)}), f32[8,16,128]{2,1,0:T(8,128)S(1)}, u32[]{:S(2)}, u32[]{:S(2)}) async-start(f32[8,16,128]{2,1,0:T(8,128)} %get-tuple-element.52), calls=%async_computation.5 | async-start | bytes 131072 | tf_op jit(solution)/shard_map/all_to_all | solution.py:57
  191.4 0.7 iota_compare_fusion.4
  192.1 0.6 gather_fusion.2
  192.7 4.5 %all-to-all-done.4 = f32[8,16,128]{2,1,0:T(8,128)S(1)} async-done(((f32[8,16,128]{2,1,0:T(8,128)}), f32[8,16,128]{2,1,0:T(8,128)S(1)}, u32[]{:S(2)}, u32[]{:S(2)}) %all-to-all-start.4) | async-done | bytes 65568 | tf_op jit(solution)/shard_map/all_to_all | solution.py:57
  197.2 0.6 gather_fusion.9
  197.9 0.9 divide_select_fusion.2
  198.8 0.6 gather_fusion.10
  199.5 8.6 %multiply_reduce_fusion.1 = f32[8,16,128]{2,1,0:T(8,128)} fusion(f32[8,16,128,256]{3,2,1,0:T(8,128)} %get-tuple-element.32, f32[8,16,256]{2,1,0:T(8,128)S(1)} %bitcast.65), kind=kLoop, calls=%fused_computation.21 | loop fusion | flops 8372224 | bytes 16973824 | tf_op jit(solution)/shard_map/reduce_sum | solution.py:80
  208.4 39.3 %all-reduce.6.cloned.1.call-done = f32[128,128]{1,0:T(8,128)} async-done(((f32[128,128]{1,0:T(8,128)}), f32[128,128]{1,0:T(8,128)}) %all-reduce.6.cloned.1.call-update) | async-done | bytes 65552 | tf_op jit(solution)/shard_map/psum | solution.py:81
  247.7 0.9 divide_select_fusion.1
  248.6 0.6 gather_fusion.11
  249.2 8.6 %multiply_reduce_fusion = f32[8,16,128]{2,1,0:T(8,128)} fusion(f32[8,16,128,256]{3,2,1,0:T(8,128)} %get-tuple-element.32, f32[8,16,256]{2,1,0:T(8,128)S(1)} %bitcast.64), kind=kLoop, calls=%fused_computation.20 | loop fusion | flops 8372224 | bytes 16973824 | tf_op jit(solution)/shard_map/reduce_sum | solution.py:80
  257.9 42.0 %all-reduce.8.cloned.1.call-done = f32[128,128]{1,0:T(8,128)} async-done(((f32[128,128]{1,0:T(8,128)}), f32[128,128]{1,0:T(8,128)}) %all-reduce.8.cloned.1.call-update) | async-done | bytes 65552 | tf_op jit(solution)/shard_map/psum | solution.py:81
  299.9 0.9 divide_select_fusion
  300.8 0.6 gather_fusion.12
  301.5 0.7 broadcast_select_fusion.2
  302.2 4.6 %all-to-all-start.5 = ((f32[8,16,128]{2,1,0:T(8,128)}), f32[8,16,128]{2,1,0:T(8,128)S(1)}, u32[]{:S(2)}, u32[]{:S(2)}) async-start(f32[8,16,128]{2,1,0:T(8,128)} %broadcast_select_fusion.2), calls=%async_computation.6 | async-start | bytes 131072 | tf_op jit(solution)/shard_map/all_to_all | solution.py:84
  306.8 5.9 %all-to-all-done.5 = f32[8,16,128]{2,1,0:T(8,128)S(1)} async-done(((f32[8,16,128]{2,1,0:T(8,128)}), f32[8,16,128]{2,1,0:T(8,128)S(1)}, u32[]{:S(2)}, u32[]{:S(2)}) %all-to-all-start.5) | async-done | bytes 65568 | tf_op jit(solution)/shard_map/all_to_all | solution.py:84
  312.7 1.2 gather_fusion.13
  (59 shorter events, 1.7 us)
Async XLA Ops:
  6.5 1.9 copy-start
  6.5 21.9 %copy-start.2 = (f32[1,64,128]{2,1,0:T(8,128)S(1)}, f32[1,64,128]{2,1,0:T(8,128)}, u32[]{:S(2)}) copy-start(f32[1,64,128]{2,1,0:T(8,128)} %param.11) | copy-start | bytes 98308
  6.5 21.9 %copy-start.3 = (s32[64,128]{1,0:T(8,128)S(1)}, s32[64,128]{1,0:T(8,128)}, u32[]{:S(2)}) copy-start(s32[64,128]{1,0:T(8,128)} %param.12) | copy-start | bytes 98308
  6.5 22.6 %copy-start.1 = (f32[1,64,128]{2,1,0:T(8,128)S(1)}, f32[1,64,128]{2,1,0:T(8,128)}, u32[]{:S(2)}) copy-start(f32[1,64,128]{2,1,0:T(8,128)} %param.10) | copy-start | bytes 98308
  6.5 42.3 %reduce-scatter.2.cloned.1.call-start = ((), (), s32[]{:S(2)}) async-start(), calls=%async_computation.7 | async-start | bytes 2621440 | tf_op jit(solution)/shard_map/reduce_scatter | solution.py:52
  13.1 11.9 %all-to-all-start = ((s32[8,16,1]{1,2,0:T(1,128)}), s32[8,16,1]{1,2,0:T(1,128)S(1)}, u32[]{:S(2)}, u32[]{:S(2)}) async-start(s32[8,16,1]{1,2,0:T(1,128)} %bitcast.3), calls=%async_computation | async-start | bytes 8192 | tf_op jit(solution)/shard_map/all_to_all | solution.py:62
  24.9 18.8 %all-to-all-start.2 = ((s32[128,8,128]{2,1,0:T(8,128)}), s32[128,8,128]{2,1,0:T(8,128)S(1)}, u32[]{:S(2)}, u32[]{:S(2)}) async-start(s32[128,8,128]{2,1,0:T(8,128)} %constant_dynamic-slice_fusion), calls=%async_computation.2 | async-start | bytes 1048576 | tf_op jit(solution)/shard_map/all_to_all | solution.py:61
  48.9 19.9 %all-to-all-start.3 = ((f32[128,8,128]{2,1,0:T(8,128)}), f32[128,8,128]{2,1,0:T(8,128)S(1)}, u32[]{:S(2)}, u32[]{:S(2)}) async-start(f32[128,8,128]{2,1,0:T(8,128)} %reduce-scatter.2.cloned.1.call-done), calls=%async_computation.4 | async-start | bytes 1048576 | tf_op jit(solution)/shard_map/all_to_all | solution.py:56
  53.5 124.0 %all-reduce.10.cloned.1.call-start = ((), (), s32[]{:S(2)}) async-start(), calls=%async_computation.10 | async-start | bytes 393216 | tf_op jit(solution)/shard_map/psum | solution.py:81
  188.0 9.2 %all-to-all-start.4 = ((f32[8,16,128]{2,1,0:T(8,128)}), f32[8,16,128]{2,1,0:T(8,128)S(1)}, u32[]{:S(2)}, u32[]{:S(2)}) async-start(f32[8,16,128]{2,1,0:T(8,128)} %get-tuple-element.52), calls=%async_computation.5 | async-start | bytes 131072 | tf_op jit(solution)/shard_map/all_to_all | solution.py:57
  191.4 56.3 %all-reduce.6.cloned.1.call-start = ((), (), s32[]{:S(2)}) async-start(), calls=%async_computation.8 | async-start | bytes 131072 | tf_op jit(solution)/shard_map/psum | solution.py:81
  199.5 107.3 %copy-start.4 = (s32[64,1]{0,1:T(1,128)S(1)}, s32[64,1]{0,1:T(1,128)}, u32[]{:S(2)}) copy-start(s32[64,1]{0,1:T(1,128)} %param.14) | copy-start | bytes 772
  208.1 91.7 %all-reduce.8.cloned.1.call-start = ((), (), s32[]{:S(2)}) async-start(), calls=%async_computation.9 | async-start | bytes 131072 | tf_op jit(solution)/shard_map/psum | solution.py:81
  302.2 10.5 %all-to-all-start.5 = ((f32[8,16,128]{2,1,0:T(8,128)}), f32[8,16,128]{2,1,0:T(8,128)S(1)}, u32[]{:S(2)}, u32[]{:S(2)}) async-start(f32[8,16,128]{2,1,0:T(8,128)} %broadcast_select_fusion.2), calls=%async_computation.6 | async-start | bytes 131072 | tf_op jit(solution)/shard_map/all_to_all | solution.py:84
Sparse Core Ops, SparseCore 0:
  10.9 37.9 reduce-scatter.1
  136.4 41.0 all-reduce.9
  208.3 39.3 all-reduce.5
  258.0 41.8 all-reduce.7
where the time goes:
time: 321 us; the launch traced here: 320 us
  waiting for transfers between devices  163 us (51%)
  other arithmetic  82.2 us (26%)
  local copies, waits for them, and re-layouts  27.1 us (8%)
  starting transfers between devices  22.7 us (7%)
  between operations  14.7 us (5%)
  blocking collectives  10.5 us (3%)
    psum x3, waiting for transfers between devices, on_device(): summed = lax.psum(partial_sum, 'src')  123 us
    reduce_sum x8, other arithmetic, build(): return jnp.sum(picked, axis=1)  45.3 us
    reduce_sum x3, other arithmetic, on_device(): partial_sum = jnp.sum(dense * nearby[:, None, :], axis=2)  25.9 us
    all_to_all x1, waiting for transfers between devices, on_device(): lax.all_to_all(part_vals, 'blk', split_axis=0, concat_axis=0, tiled=True)  13.3 us
    dynamic_update_slice x8, local copies, waits for them, and re-layouts, tile_matrix(): dense = lax.map(build, (grouped_vals, grouped_lanes))  12.3 us
    all_to_all x1, blocking collectives, on_device(): lax.all_to_all(sum_rhs, 'blk', split_axis=0, concat_axis=0, tiled=True)  10.5 us
    all_to_all x1, waiting for transfers between devices, on_device(): lax.all_to_all(part_cols, 'blk', split_axis=0, concat_axis=0, tiled=True)  9.16 us
  transfers between devices with their start and end apart: 9, of which 9 were waited for; matrix products, arithmetic and copies ran while one was open for 4% of the time, Pallas kernels for 0%

commit v1 on v0

v1 whole, which is shorter than its diff:
```python
import functools
import jax
import jax.numpy as jnp
from jax import lax
from jax.experimental import pallas as pl
from jax.experimental.pallas import tpu as pltpu
from jax.sharding import PartitionSpec as P

SWEEPS = 3
FAR = 3.0e38


def kernel(n_src, n_blk, values_hbm, columns_hbm, diag_ref, rhs_ref, map_ref, dest_ref, keys_ref, out_ref,
           vals, cols, comb_all, comb_sum, diag_in, rhs_in, own, zed, picked, nxt, prod, prod_in,
           load_sem, comb_send, comb_recv, dr_send, dr_recv, own_send, own_recv, zed_send, zed_recv,
           nxt_send, nxt_recv, prod_send, prod_recv):
    s = lax.axis_index("src")
    b = lax.axis_index("blk")
    tiles, rows = diag_ref.shape
    stored = vals.shape[1]
    q = tiles // n_src
    lanes = n_blk * q
    total = n_blk * tiles
    src_peers = [lax.rem(s + o, n_src) for o in range(1, n_src)]
    blk_peers = [lax.rem(b + o, n_blk) for o in range(1, n_blk)]
    mesh_id = pl.DeviceIdType.MESH
    started = []

    load_v = pltpu.make_async_copy(values_hbm, vals, load_sem.at[0])
    load_c = pltpu.make_async_copy(columns_hbm, cols, load_sem.at[1])
    load_c.start()
    load_v.start()

    barrier = pltpu.get_barrier_semaphore()
    for peer in src_peers:
        pl.semaphore_signal(barrier, inc=1, device_id={"src": peer}, device_id_type=mesh_id)
    for peer in blk_peers:
        pl.semaphore_signal(barrier, inc=1, device_id={"blk": peer}, device_id_type=mesh_id)

    dest_row = dest_ref[...].astype(jnp.float32)
    comb_row = dest_row * total + keys_ref[...].astype(jnp.float32) + 1.0
    eye = lax.broadcasted_iota(jnp.int32, (tiles, tiles), 0) == lax.broadcasted_iota(jnp.int32, (tiles, tiles), 1)
    comb_col = jnp.sum(jnp.where(eye, comb_row, 0.0), axis=1, keepdims=True)
    low_col = jnp.sum(jnp.where(eye, dest_row, 0.0), axis=1, keepdims=True) * total + 1.0
    at_lane = lax.broadcasted_iota(jnp.int32, (q, lanes), 1) - b * q == lax.broadcasted_iota(jnp.int32, (q, lanes), 0)
    for part in range(n_src):
        spread = jnp.where(at_lane, comb_col[part * q:(part + 1) * q], 0.0)
        comb_all[b, part:part + 1, :] = jnp.sum(spread, axis=0, keepdims=True)

    pl.semaphore_wait(barrier, n_src + n_blk - 2)

    def send(src, dst, send_sem, recv_sem, device):
        copy = pltpu.make_async_remote_copy(src_ref=src, dst_ref=dst, send_sem=send_sem, recv_sem=recv_sem,
                                            device_id=device, device_id_type=mesh_id)
        copy.start()
        started.append(copy)

    def arrive(dst, send_sem, recv_sem, device):
        pltpu.make_async_remote_copy(src_ref=dst, dst_ref=dst, send_sem=send_sem, recv_sem=recv_sem,
                                     device_id=device, device_id_type=mesh_id).wait_recv()

    def rows_of(part):
        return pl.ds(pl.multiple_of(part * q, q), q)

    for peer in src_peers:
        send(diag_ref.at[rows_of(peer)], diag_in.at[s], dr_send.at[0, peer], dr_recv.at[0, s], {"src": peer})
        send(rhs_ref.at[rows_of(peer)], rhs_in.at[s], dr_send.at[1, peer], dr_recv.at[1, s], {"src": peer})
    for peer in blk_peers:
        send(comb_all.at[b], comb_all.at[b], comb_send.at[peer], comb_recv.at[b], {"blk": peer})

    mine = rows_of(s)
    diag_q = diag_ref[mine, :]
    owner_q = map_ref[mine, :]
    right_q = jnp.where(owner_q == s, rhs_ref[mine, :], 0.0)
    for peer in src_peers:
        arrive(diag_in.at[peer], dr_send.at[0, peer], dr_recv.at[0, peer], {"src": peer})
        diag_q = diag_q + diag_in[peer]
        arrive(rhs_in.at[peer], dr_send.at[1, peer], dr_recv.at[1, peer], {"src": peer})
        right_q = jnp.where(owner_q == peer, rhs_in[peer], right_q)

    def share(step, x_q, over_blk):
        own[step, mine, :] = x_q
        if over_blk:
            zed[step, b] = x_q
            for peer in blk_peers:
                send(zed.at[step, b], zed.at[step, b], zed_send.at[step, peer], zed_recv.at[step, b], {"blk": peer})
        for peer in src_peers:
            send(own.at[step, mine], own.at[step, mine], own_send.at[step, peer], own_recv.at[step, s], {"src": peer})

    def own_arrive(step):
        for peer in src_peers:
            arrive(own.at[step, rows_of(peer)], own_send.at[step, peer], own_recv.at[step, peer], {"src": peer})

    def product(step, take, which, first):
        def block(t, carry):
            code = cols[t]
            x = jnp.broadcast_to(take(t), (stored, rows))
            near = jnp.take_along_axis(x, code & (rows - 1), axis=1, mode="promise_in_bounds")
            hit = (code & rows) != 0
            term = jnp.where(hit if which else ~hit, near * vals[t], 0.0)
            row = jnp.sum(term, axis=0, keepdims=True)
            if first:
                prod[step, pl.ds(t, 1), :] = row
            else:
                prod[step, pl.ds(t, 1), :] = prod[step, pl.ds(t, 1), :] + row
            return carry

        lax.fori_loop(0, tiles, block, 0, unroll=8)

    share(0, right_q / diag_q, True)

    for peer in blk_peers:
        arrive(comb_all.at[peer], comb_send.at[peer], comb_recv.at[peer], {"blk": peer})
    all_combs = comb_all[0]
    for other in range(1, n_blk):
        all_combs = all_combs + comb_all[other]
    comb_sum[...] = all_combs
    after = jnp.full((tiles, 1), FAR, jnp.float32)
    least = jnp.full((tiles, 1), FAR, jnp.float32)
    for part in range(n_src):
        line = comb_sum[part:part + 1, :]
        later = (line > comb_col) & (line < low_col + total)
        after = jnp.minimum(after, jnp.min(jnp.where(later, line, FAR), axis=1, keepdims=True))
        least = jnp.minimum(least, jnp.min(jnp.where(line >= low_col, line, FAR), axis=1, keepdims=True))
    follow = jnp.where(after < FAR, after, least)
    choice = jnp.where(comb_sum[pl.ds(s, 1), :] == follow, 1.0, 0.0).astype(jnp.bfloat16)

    load_c.wait()
    load_v.wait()
    for step in range(SWEEPS - 1):
        own_arrive(step)
        product(step, lambda t: own[step, pl.ds(t, 1), :], False, True)
        for peer in blk_peers:
            arrive(zed.at[step, peer], zed_send.at[step, peer], zed_recv.at[step, peer], {"blk": peer})
        spread = zed[step].reshape(lanes, rows)
        high = spread.astype(jnp.bfloat16)
        rest = spread - high.astype(jnp.float32)
        middle = rest.astype(jnp.bfloat16)
        small = (rest - middle.astype(jnp.float32)).astype(jnp.bfloat16)
        got = jnp.dot(choice, high, preferred_element_type=jnp.float32)
        got = got + jnp.dot(choice, middle, preferred_element_type=jnp.float32)
        got = got + jnp.dot(choice, small, preferred_element_type=jnp.float32)
        picked[step] = got
        for peer in src_peers:
            send(picked.at[step], nxt.at[step, s], nxt_send.at[step, peer], nxt_recv.at[step, s], {"src": peer})
        for peer in src_peers:
            arrive(nxt.at[step, peer], nxt_send.at[step, peer], nxt_recv.at[step, peer], {"src": peer})
            got = got + nxt[step, peer]
        nxt[step, s] = got
        product(step, lambda t: nxt[step, s, pl.ds(t, 1), :], True, False)
        for peer in src_peers:
            send(prod.at[step, rows_of(peer)], prod_in.at[step, s], prod_send.at[step, peer], prod_recv.at[step, s], {"src": peer})
        summed = prod[step, mine, :]
        for peer in src_peers:
            arrive(prod_in.at[step, peer], prod_send.at[step, peer], prod_recv.at[step, peer], {"src": peer})
            summed = summed + prod_in[step, peer]
        share(step + 1, (right_q - summed) / diag_q, step < SWEEPS - 2)
    own_arrive(SWEEPS - 1)
    out_ref[...] = own[SWEEPS - 1]
    for copy in started:
        copy.wait_send()


def on_device(values, diagonal, rhs_parts, owner_map, columns, destination, order_keys):
    n_src = lax.axis_size("src")
    n_blk = lax.axis_size("blk")
    tiles, rows = diagonal.shape[1:]
    stored = values.shape[2]
    q = tiles // n_src
    f32 = jnp.float32
    dma = pltpu.SemaphoreType.DMA
    small = pl.BlockSpec(memory_space=pltpu.VMEM)
    big = pl.BlockSpec(memory_space=pl.ANY)
    return pl.pallas_call(
        functools.partial(kernel, n_src, n_blk),
        out_shape=jax.ShapeDtypeStruct((tiles, rows), f32),
        in_specs=[big, big, small, small, small, small, small],
        out_specs=small,
        scratch_shapes=[
            pltpu.VMEM((tiles, stored, rows), f32),
            pltpu.VMEM((tiles, stored, rows), jnp.int32),
            pltpu.VMEM((n_blk, n_src, n_blk * q), f32),
            pltpu.VMEM((n_src, n_blk * q), f32),
            pltpu.VMEM((n_src, q, rows), f32),
            pltpu.VMEM((n_src, q, rows), f32),
            pltpu.VMEM((SWEEPS, tiles, rows), f32),
            pltpu.VMEM((SWEEPS - 1, n_blk, q, rows), f32),
            pltpu.VMEM((SWEEPS - 1, tiles, rows), f32),
            pltpu.VMEM((SWEEPS - 1, n_src, tiles, rows), f32),
            pltpu.VMEM((SWEEPS - 1, tiles, rows), f32),
            pltpu.VMEM((SWEEPS - 1, n_src, q, rows), f32),
            dma((2,)),
            dma((n_blk,)), dma((n_blk,)),
            dma((2, n_src)), dma((2, n_src)),
            dma((SWEEPS, n_src)), dma((SWEEPS, n_src)),
            dma((SWEEPS - 1, n_blk)), dma((SWEEPS - 1, n_blk)),
            dma((SWEEPS - 1, n_src)), dma((SWEEPS - 1, n_src)),
            dma((SWEEPS - 1, n_src)), dma((SWEEPS - 1, n_src)),
        ],
        compiler_params=pltpu.CompilerParams(collective_id=0, has_side_effects=True),
    )(values[0], columns, diagonal[0], rhs_parts[0], owner_map, destination.reshape(1, tiles), order_keys.reshape(1, tiles))


def solution(mesh):
    placed = (
        P("src", "blk", None, None),
        P("src", "blk", None),
        P("src", "blk", None),
        P("blk", None),
        P("blk", None, None),
        P("blk", None),
        P("blk"),
    )
    return jax.shard_map(
        on_device, mesh=mesh, in_specs=placed, out_specs=P("blk", None), check_vma=False
    )
```

time: 321 us -> 41.6 us (0.13)
  waiting for transfers between devices: 163 us -> 0 us
  other arithmetic: 82.2 us -> 0 us
  Pallas kernels: 0 us -> 39.9 us
  local copies, waits for them, and re-layouts: 27.1 us -> 1.38 us
  starting transfers between devices: 22.7 us -> 0 us
  between operations: 14.7 us -> 0.01 us
  blocking collectives: 10.5 us -> 0 us
    psum x3 -> x0, waiting for transfers between devices: 123 us -> none  [on_device(): summed = lax.psum(partial_sum, 'src')]
    reduce_sum x16 -> x0, other arithmetic: 73.1 us -> none  [the longest x8 45.3 us: build(): return jnp.sum(picked, axis=1)]
    pallas_call x0 -> x1, Pallas kernels: none -> 39.9 us  [on_device(): pl.pallas_call(functools.partial(kernel, n_src, n_blk), out_shape=jax.Sha...]
    all_to_all x5 -> x0, waiting for transfers between devices: 35.3 us -> none  [the longest x1 13.3 us: on_device(): lax.all_to_all(part_vals, 'blk', split_axis=0, concat_axis=0, tiled=True)]
    all_to_all x5 -> x0, starting transfers between devices: 22.4 us -> none  [the longest x1 6.35 us: on_device(): lax.all_to_all(send_keys, 'blk', split_axis=0, concat_axis=0, tiled=True)]
    gather x14 -> x0, local copies, waits for them, and re-layouts: 12.4 us -> none  [the longest x1 2.17 us: on_device(): send_cols = columns[source_tile]]
    dynamic_update_slice x8 -> x0, local copies, waits for them, and re-layouts: 12.3 us -> none  [tile_matrix(): dense = lax.map(build, (grouped_vals, grouped_lanes))]
    all_to_all x1 -> x0, blocking collectives: 10.5 us -> none  [on_device(): lax.all_to_all(sum_rhs, 'blk', split_axis=0, concat_axis=0, tiled=True)]
  transfers between devices with their start and end apart: 9 -> 0, of which waited for: 9 -> 0; matrix products, arithmetic and copies ran while one was open for 4% -> 0% of each run, Pallas kernels for 0% -> 0%
where the time goes in v1:
time: 41.6 us; the launch traced here: 41.3 us
  Pallas kernels  39.9 us (96%)
  local copies, waits for them, and re-layouts  1.38 us (3%)
    pallas_call x1, Pallas kernels, on_device(): pl.pallas_call(functools.partial(kernel, n_src, n_blk), out_shape=jax.Sha...  39.9 us
    unnamed x1, local copies, waits for them, and re-layouts  1.38 us

profile of v1, /device:TPU:0, one launch (start us, length us, event | category | flops | bytes accessed | tf_op | source)
XLA Modules:
  0.0 41.3 jit_solution(11220321360464397227)
XLA Ops:
  0.0 39.9 %shard_map.73 = f32[64,128]{1,0:T(8,128)} custom-call(f32[64,32,128]{2,1,0:T(8,128)} %bitcast.5, s32[64,32,128]{2,1,0:T(8,128)} %columns_hbm.1, f32[64,128]{1,0:T(8,128)} %bitcast.6, f32[64,128]{1,0:T(8,128)} %bitcast.7, s32[64,128]{1,0:T(8,128)} %map_ref.1, s32[1,64]{1,0:T(1,128)} %bitcast.8, s32[1,64]{1,0:T(1,128)} %bitcast.9), custom_call_target="tpu_custom_call" | custom-call | tf_op jit(solution)/shard_map/pallas_call | solution.py:174
  39.9 1.4 %copy.9 = f32[64,128]{1,0:T(8,128)} copy(f32[64,128]{1,0:T(8,128)} %shard_map.73) | data formatting | bytes 65536

commit v2 on v1

v2 whole, which is shorter than its diff:
```python
import functools
import jax
import jax.numpy as jnp
from jax import lax
from jax.experimental import pallas as pl
from jax.experimental.pallas import tpu as pltpu
from jax.sharding import PartitionSpec as P

SWEEPS = 3
FAR = 3.0e38
CHUNKS = 4
CUTS = (1, 3)


def kernel(n_src, n_blk, values_hbm, columns_hbm, diag_hbm, rhs_hbm, map_hbm, dest_hbm, keys_hbm, out_ref,
           vals, mat_in, cols, diag_ref, rhs_ref, map_ref, dest_ref, keys_ref,
           comb_all, comb_sum, diag_in, rhs_in, zed, picked, nxt, prod, fin,
           load_sem, comb_send, comb_recv, dr_send, dr_recv, out_send, out_recv, zed_send, zed_recv,
           nxt_send, nxt_recv, mat_send, mat_recv):
    s = lax.axis_index("src")
    b = lax.axis_index("blk")
    tiles, rows = diag_ref.shape
    stored = vals.shape[1]
    q = tiles // n_src
    lanes = n_blk * q
    total = n_blk * tiles
    chunk = q // CHUNKS
    src_peers = [lax.rem(s + o, n_src) for o in range(1, n_src)]
    blk_peers = [lax.rem(b + o, n_blk) for o in range(1, n_blk)]
    mesh_id = pl.DeviceIdType.MESH
    started = []

    def rows_of(part):
        return pl.ds(pl.multiple_of(part * q, q), q)

    mine = rows_of(s)
    barrier = pltpu.get_barrier_semaphore()
    for peer in src_peers:
        pl.semaphore_signal(barrier, inc=1, device_id={"src": peer}, device_id_type=mesh_id)
    for peer in blk_peers:
        pl.semaphore_signal(barrier, inc=1, device_id={"blk": peer}, device_id_type=mesh_id)
    pairs = [(dest_hbm, dest_ref), (keys_hbm, keys_ref), (diag_hbm, diag_ref), (rhs_hbm, rhs_ref), (map_hbm, map_ref),
             (columns_hbm.at[mine], cols), (values_hbm.at[mine], vals)]
    loads = [pltpu.make_async_copy(src, dst, load_sem.at[i]) for i, (src, dst) in enumerate(pairs)]
    for load in loads:
        load.start()
    for load in loads[:2]:
        load.wait()

    dest_row = dest_ref[...].astype(jnp.float32)
    comb_row = dest_row * total + keys_ref[...].astype(jnp.float32) + 1.0
    eye = lax.broadcasted_iota(jnp.int32, (tiles, tiles), 0) == lax.broadcasted_iota(jnp.int32, (tiles, tiles), 1)
    comb_col = jnp.sum(jnp.where(eye, comb_row, 0.0), axis=1, keepdims=True)
    low_col = jnp.sum(jnp.where(eye, dest_row, 0.0), axis=1, keepdims=True) * total + 1.0
    at_lane = lax.broadcasted_iota(jnp.int32, (q, lanes), 1) - b * q == lax.broadcasted_iota(jnp.int32, (q, lanes), 0)
    for part in range(n_src):
        spread = jnp.where(at_lane, comb_col[part * q:(part + 1) * q], 0.0)
        comb_all[b, part:part + 1, :] = jnp.sum(spread, axis=0, keepdims=True)
    for load in loads[2:5]:
        load.wait()

    pl.semaphore_wait(barrier, n_src + n_blk - 2)

    def send(src, dst, send_sem, recv_sem, device):
        copy = pltpu.make_async_remote_copy(src_ref=src, dst_ref=dst, send_sem=send_sem, recv_sem=recv_sem,
                                            device_id=device, device_id_type=mesh_id)
        copy.start()
        started.append(copy)

    def arrive(dst, send_sem, recv_sem, device):
        pltpu.make_async_remote_copy(src_ref=dst, dst_ref=dst, send_sem=send_sem, recv_sem=recv_sem,
                                     device_id=device, device_id_type=mesh_id).wait_recv()

    def send_matrix(low, high):
        for piece in range(low, high):
            for peer in src_peers:
                there = pl.ds(pl.multiple_of(peer * q + piece * chunk, chunk), chunk)
                here = pl.ds(piece * chunk, chunk)
                send(values_hbm.at[there], mat_in.at[s, here], mat_send.at[piece, peer], mat_recv.at[piece, s], {"src": peer})

    for peer in src_peers:
        send(diag_ref.at[rows_of(peer)], diag_in.at[s], dr_send.at[0, peer], dr_recv.at[0, s], {"src": peer})
        send(rhs_ref.at[rows_of(peer)], rhs_in.at[s], dr_send.at[1, peer], dr_recv.at[1, s], {"src": peer})
    for peer in blk_peers:
        send(comb_all.at[b], comb_all.at[b], comb_send.at[peer], comb_recv.at[b], {"blk": peer})
    send_matrix(0, CUTS[0])

    diag_q = diag_ref[mine, :]
    owner_q = map_ref[mine, :]
    right_q = jnp.where(owner_q == s, rhs_ref[mine, :], 0.0)
    for peer in src_peers:
        arrive(diag_in.at[peer], dr_send.at[0, peer], dr_recv.at[0, peer], {"src": peer})
        diag_q = diag_q + diag_in[peer]
        arrive(rhs_in.at[peer], dr_send.at[1, peer], dr_recv.at[1, peer], {"src": peer})
        right_q = jnp.where(owner_q == peer, rhs_in[peer], right_q)

    def share(step, x_q):
        zed[step, b] = x_q
        for peer in blk_peers:
            send(zed.at[step, b], zed.at[step, b], zed_send.at[step, peer], zed_recv.at[step, b], {"blk": peer})

    def product(step):
        def block(t, carry):
            code = cols[t]
            if step == 0:
                entry = vals[t]
                for peer in src_peers:
                    entry = entry + mat_in[peer, t]
                vals[t] = entry
            else:
                entry = vals[t]
            lane = code & (rows - 1)
            x = jnp.broadcast_to(zed[step, b, pl.ds(t, 1), :], (stored, rows))
            y = jnp.broadcast_to(nxt[step, s, pl.ds(t, 1), :], (stored, rows))
            near = jnp.take_along_axis(x, lane, axis=1, mode="promise_in_bounds")
            far = jnp.take_along_axis(y, lane, axis=1, mode="promise_in_bounds")
            term = jnp.where((code & rows) != 0, far, near) * entry
            prod[pl.ds(t, 1), :] = jnp.sum(term, axis=0, keepdims=True)
            return carry

        lax.fori_loop(0, q, block, 0, unroll=8)
        return prod[...]

    share(0, right_q / diag_q)
    send_matrix(CUTS[0], CUTS[1])

    for peer in blk_peers:
        arrive(comb_all.at[peer], comb_send.at[peer], comb_recv.at[peer], {"blk": peer})
    all_combs = comb_all[0]
    for other in range(1, n_blk):
        all_combs = all_combs + comb_all[other]
    comb_sum[...] = all_combs
    after = jnp.full((tiles, 1), FAR, jnp.float32)
    least = jnp.full((tiles, 1), FAR, jnp.float32)
    for part in range(n_src):
        line = comb_sum[part:part + 1, :]
        later = (line > comb_col) & (line < low_col + total)
        after = jnp.minimum(after, jnp.min(jnp.where(later, line, FAR), axis=1, keepdims=True))
        least = jnp.minimum(least, jnp.min(jnp.where(line >= low_col, line, FAR), axis=1, keepdims=True))
    follow = jnp.where(after < FAR, after, least)
    choice = jnp.where(comb_sum[pl.ds(s, 1), :] == follow, 1.0, 0.0).astype(jnp.bfloat16)

    for step in range(SWEEPS - 1):
        for peer in blk_peers:
            arrive(zed.at[step, peer], zed_send.at[step, peer], zed_recv.at[step, peer], {"blk": peer})
        spread = zed[step].reshape(lanes, rows)
        high = spread.astype(jnp.bfloat16)
        rest = spread - high.astype(jnp.float32)
        middle = rest.astype(jnp.bfloat16)
        small = (rest - middle.astype(jnp.float32)).astype(jnp.bfloat16)
        got = jnp.dot(choice, high, preferred_element_type=jnp.float32)
        got = got + jnp.dot(choice, middle, preferred_element_type=jnp.float32)
        got = got + jnp.dot(choice, small, preferred_element_type=jnp.float32)
        picked[step] = got
        for peer in src_peers:
            send(picked.at[step, rows_of(peer)], nxt.at[step, s], nxt_send.at[step, peer], nxt_recv.at[step, s], {"src": peer})
        if step == 0:
            send_matrix(CUTS[1], CHUNKS)
            for load in loads[5:]:
                load.wait()
        ahead = picked[step, mine, :]
        for peer in src_peers:
            arrive(nxt.at[step, peer], nxt_send.at[step, peer], nxt_recv.at[step, peer], {"src": peer})
            ahead = ahead + nxt[step, peer]
        nxt[step, s] = ahead
        if step == 0:
            for piece in range(CHUNKS):
                for peer in src_peers:
                    here = pl.ds(piece * chunk, chunk)
                    arrive(mat_in.at[peer, here], mat_send.at[piece, peer], mat_recv.at[piece, peer], {"src": peer})
        x_q = (right_q - product(step)) / diag_q
        if step < SWEEPS - 2:
            share(step + 1, x_q)
    fin[mine, :] = x_q
    for peer in src_peers:
        send(fin.at[mine], fin.at[mine], out_send.at[peer], out_recv.at[s], {"src": peer})
    for peer in src_peers:
        arrive(fin.at[rows_of(peer)], out_send.at[peer], out_recv.at[peer], {"src": peer})
    out_ref[...] = fin[...]
    for copy in started:
        copy.wait_send()


def on_device(values, diagonal, rhs_parts, owner_map, columns, destination, order_keys):
    n_src = lax.axis_size("src")
    n_blk = lax.axis_size("blk")
    tiles, rows = diagonal.shape[1:]
    stored = values.shape[2]
    q = tiles // n_src
    f32 = jnp.float32
    i32 = jnp.int32
    dma = pltpu.SemaphoreType.DMA
    later = SWEEPS - 1
    return pl.pallas_call(
        functools.partial(kernel, n_src, n_blk),
        out_shape=pltpu.VMEM((tiles, rows), f32),
        in_specs=[pl.BlockSpec(memory_space=pl.ANY)] * 7,
        out_specs=pl.BlockSpec(memory_space=pltpu.VMEM),
        scratch_shapes=[
            pltpu.VMEM((q, stored, rows), f32),
            pltpu.VMEM((n_src, q, stored, rows), f32),
            pltpu.VMEM((q, stored, rows), i32),
            pltpu.VMEM((tiles, rows), f32),
            pltpu.VMEM((tiles, rows), f32),
            pltpu.VMEM((tiles, rows), i32),
            pltpu.VMEM((1, tiles), i32),
            pltpu.VMEM((1, tiles), i32),
            pltpu.VMEM((n_blk, n_src, n_blk * q), f32),
            pltpu.VMEM((n_src, n_blk * q), f32),
            pltpu.VMEM((n_src, q, rows), f32),
            pltpu.VMEM((n_src, q, rows), f32),
            pltpu.VMEM((later, n_blk, q, rows), f32),
            pltpu.VMEM((later, tiles, rows), f32),
            pltpu.VMEM((later, n_src, q, rows), f32),
            pltpu.VMEM((q, rows), f32),
            pltpu.VMEM((tiles, rows), f32),
            dma((7,)),
            dma((n_blk,)), dma((n_blk,)),
            dma((2, n_src)), dma((2, n_src)),
            dma((n_src,)), dma((n_src,)),
            dma((later, n_blk)), dma((later, n_blk)),
            dma((later, n_src)), dma((later, n_src)),
            dma((CHUNKS, n_src)), dma((CHUNKS, n_src)),
        ],
        compiler_params=pltpu.CompilerParams(collective_id=0, has_side_effects=True),
    )(values[0], columns, diagonal[0], rhs_parts[0], owner_map, destination.reshape(1, tiles), order_keys.reshape(1, tiles))


def solution(mesh):
    placed = (
        P("src", "blk", None, None),
        P("src", "blk", None),
        P("src", "blk", None),
        P("blk", None),
        P("blk", None, None),
        P("blk", None),
        P("blk"),
    )
    return jax.shard_map(
        on_device, mesh=mesh, in_specs=placed, out_specs=P("blk", None), check_vma=False
    )
```

time: 41.6 us -> 32 us (0.77)
  Pallas kernels: 39.9 us -> 31.2 us
  local copies, waits for them, and re-layouts: 1.38 us -> 0.62 us
    pallas_call x1, Pallas kernels: 39.9 us -> 31.2 us  [on_device(): pl.pallas_call(functools.partial(kernel, n_src, n_blk), out_shape=pltpu.V...]
    unnamed x1, local copies, waits for them, and re-layouts: 1.38 us -> 0.62 us
where the time goes in v2:
time: 32 us; the launch traced here: 31.8 us
  Pallas kernels  31.2 us (98%)
  local copies, waits for them, and re-layouts  0.62 us (2%)
    pallas_call x1, Pallas kernels, on_device(): pl.pallas_call(functools.partial(kernel, n_src, n_blk), out_shape=pltpu.V...  31.2 us

profile of v2, /device:TPU:0, one launch (start us, length us, event | category | flops | bytes accessed | tf_op | source)
XLA Modules:
  0.0 31.8 jit_solution(13571674444710549409)
XLA Ops:
  0.0 31.2 %shard_map.73 = f32[64,128]{1,0:T(8,128)S(1)} custom-call(f32[64,32,128]{2,1,0:T(8,128)} %bitcast.5, s32[64,32,128]{2,1,0:T(8,128)} %columns_hbm.1, f32[64,128]{1,0:T(8,128)} %bitcast.6, f32[64,128]{1,0:T(8,128)} %bitcast.7, s32[64,128]{1,0:T(8,128)} %map_hbm.1, s32[1,64]{1,0:T(1,128)} %bitcast.8, s32[1,64]{1,0:T(1,128)} %bitcast.9), custom_call_target="tpu_custom_call" | custom-call | tf_op jit(solution)/shard_map/pallas_call | solution.py:194
  31.2 0.6 %copy.9 = f32[64,128]{1,0:T(8,128)} copy(f32[64,128]{1,0:T(8,128)S(1)} %shard_map.73) | data formatting | bytes 65536
